TPU v7x, 256 devices: a whole 4x4x8 slice. The times are simulated.
256 devices in a mesh: section: 8 (over z), dp: 32 (over x, y, core).
Axes of the slice: x: 4, y: 4, z: 8, core: 2. Of those that a mesh axis runs over, the one named last changes fastest.
Arguments:
- inject: bfloat16 [8, 256, 4096], P('section', 'dp'), may hold values from -42 to 42, as said below
- w_gate: bfloat16 [8, 4096, 11008], P('section', None, 'dp'), may hold values from -0.09375 to 0.09375
- w_up: bfloat16 [8, 4096, 11008], P('section', None, 'dp'), may hold values from -0.09375 to 0.09375
- w_down: bfloat16 [8, 11008, 4096], P('section', 'dp'), may hold values from -0.0546875 to 0.0546875
- gain: float32 [8, 4096], P('section'), may hold values from 0.5 to 1.5
Outputs:
- iterate: float32 [8, 256, 4096], P('section', 'dp')
- mixing: float32 [8, 5, 5], P('section')
Inputs may be any that keep to these rules, and one draw needn't show every extreme that they name: inject has entries of varied magnitude from token to token.
All inputs are finite; a program needn't handle non-finite values.
Results may differ from a plain program's by a relative error of at most 0.0038.
Values may be sent and summed in bfloat16 or wider, within the bound.
A program may use at most 64 MiB of HBM per device.

v0:
```python
import jax
import jax.numpy as jnp
from jax import lax
from jax.sharding import PartitionSpec as P

ITERS = 5
HIST = 5


def in_order(tiles, dim):
    tiles = jnp.moveaxis(tiles, 0, dim)
    dims = tiles.shape
    return tiles.reshape(*dims[:dim], dims[dim] * dims[dim + 1], *dims[dim + 2 :])


def copy_for_each(array, axis):
    peers = lax.axis_size(axis)
    return lax.all_to_all(
        jnp.broadcast_to(array[None], (peers, *array.shape)), axis, 0, 0, tiled=True
    )


def collect(array, axis, dim):
    return in_order(copy_for_each(array, axis), dim)


def split_up(array, dim, peers):
    dims = array.shape
    tiles = array.reshape(*dims[:dim], peers, dims[dim] // peers, *dims[dim + 1 :])
    return jnp.moveaxis(tiles, dim, 0)


def sent_and_summed(array, axis, dim):
    peers = lax.axis_size(axis)
    tiles = lax.all_to_all(split_up(array, dim, peers), axis, 0, 0, tiled=True)
    return jnp.sum(tiles.astype(jnp.float32), axis=0)


def passed_along(array, axis, by):
    peers = lax.axis_size(axis)
    return lax.ppermute(array, axis, [(i, (i + by) % peers) for i in range(peers)])


def of_everyone(array, axis):
    return copy_for_each(array, axis).sum(axis=0)


def rms_scaled(values, gain_row):
    inverse = lax.rsqrt(jnp.mean(values * values, axis=-1, keepdims=True) + 1e-06)
    return (values * inverse * gain_row).astype(jnp.bfloat16)


def solve_small(system, target):
    count = system.shape[-1]
    entries = [[system[..., i, j] for j in range(count)] for i in range(count)]
    values = [target[..., i] for i in range(count)]
    for p in range(count):
        for i in range(p + 1, count):
            factor = entries[i][p] / entries[p][p]
            for j in range(p, count):
                entries[i][j] = entries[i][j] - factor * entries[p][j]
            values[i] = values[i] - factor * values[p]
    answer = [None] * count
    for i in range(count - 1, -1, -1):
        accum = values[i]
        for j in range(i + 1, count):
            accum = accum - entries[i][j] * answer[j]
        answer[i] = accum / entries[i][i]
    return jnp.stack(answer, axis=-1)


def mixing_weights(matrix, iteration):
    live = (jnp.arange(HIST) <= iteration).astype(jnp.float32)
    damp = 0.01 * jnp.trace(matrix) / (iteration + 1) + 1e-06
    eye_mat = jnp.eye(HIST, dtype=jnp.float32)
    diagonal = live * damp + (1.0 - live)
    system = matrix * live[:, None] * live[None, :] + eye_mat * diagonal[None, :]
    beta = solve_small(system, live)
    return beta / jnp.sum(beta)


def local(inject, w_gate, w_up, w_down, gain):
    tok_rows = inject.shape[1]
    features = inject.shape[2]
    groups = lax.axis_size("dp")
    cell_count = float(tok_rows * groups * features)
    source = inject[0].astype(jnp.float32)
    gain_row = gain[0]
    gate_local = w_gate[0]
    up_local = w_up[0]
    down_local = w_down[0]
    iterate = jnp.zeros((tok_rows, features), jnp.float32)
    images = jnp.zeros((HIST, tok_rows, features), jnp.float32)
    misfits = jnp.zeros((HIST, tok_rows, features), jnp.float32)
    gram_matrix = jnp.zeros((HIST, HIST), jnp.float32)
    mixing = jnp.zeros((ITERS, HIST), jnp.float32)
    for iteration in range(ITERS):
        normed = rms_scaled(iterate, gain_row)
        segment = collect(normed, "dp", 0)
        gate_val = jnp.dot(segment, gate_local, preferred_element_type=jnp.float32)
        up_val = jnp.dot(segment, up_local, preferred_element_type=jnp.float32)
        hidden = (jax.nn.silu(gate_val) * up_val).astype(jnp.bfloat16)
        partials = jnp.dot(hidden, down_local, preferred_element_type=jnp.float32)
        summed = sent_and_summed(partials.astype(jnp.bfloat16), "dp", 0)
        output = (iterate + summed).astype(jnp.bfloat16)
        before = passed_along(output, "section", 1)
        mapped = source + 0.5 * before.astype(jnp.float32)
        misfit = mapped - iterate
        images = images.at[iteration].set(mapped)
        misfits = misfits.at[iteration].set(misfit)
        local_gram = (
            jnp.einsum("htd,gtd->hg", misfits, misfits, precision=lax.Precision.HIGHEST)
            / cell_count
        )
        gram_matrix = of_everyone(local_gram, "dp")
        weights = mixing_weights(gram_matrix, iteration)
        mixing = mixing.at[iteration].set(weights)
        iterate = jnp.einsum("h,htd->td", weights, images, precision=lax.Precision.HIGHEST)
    return (iterate[None], mixing[None])


def solution(mesh):
    placed = (
        P("section", "dp", None),
        P("section", None, "dp"),
        P("section", None, "dp"),
        P("section", "dp", None),
        P("section", None),
    )
    return jax.shard_map(
        local,
        mesh=mesh,
        in_specs=placed,
        out_specs=(P("section", "dp", None), P("section", None, None)),
        check_vma=False,
    )
```

profile of v0, /device:TPU:1, one launch (start us, length us, event | category | flops | bytes accessed | tf_op | source)
XLA Modules:
  0.0 711.8 jit_solution(1392657259811600408)
XLA Ops:
  1.8 36.8 %all_to_all.75 = bf16[32,8,4096]{2,1,0:T(8,128)(2,1)S(1)} all-to-all(bf16[32,8,4096]{2,1,0:T(8,128)(2,1)S(1)} %broadcast_in_dim.24), channel_id=1, replica_groups=mesh['section'=8,'dp'=32] {'dp'}, dimensions={0} | all-to-all | bytes 4194304 | tf_op jit(solution)/shard_map/all_to_all | solution.py:18
  38.6 1.3 copy-done.2
  39.9 1.0 fusion.28
  40.9 7.4 %fusion = bf16[32,8,4096]{2,1,0:T(8,128)(2,1)} fusion(bf16[1,344,4096]{2,1,0:T(8,128)(2,1)S(1)} %copy-done, bf16[1,4096,344]{1,2,0:T(8,128)(2,1)} %param.37, bf16[32,8,4096]{2,1,0:T(8,128)(2,1)} %copy-done.2, f32[256,344]{0,1:T(8,128)S(1)} %fusion.28), kind=kOutput, calls=%fused_computation.5 | convolution fusion | flops 1444417536 | bytes 10182656 | tf_op jit(solution)/shard_map/dot_general | solution.py:103
  48.3 32.7 %all_to_all.76 = bf16[32,8,4096]{2,1,0:T(8,128)(2,1)} all-to-all(bf16[32,8,4096]{2,1,0:T(8,128)(2,1)} %fusion), channel_id=1, replica_groups=mesh['section'=8,'dp'=32] {'dp'}, dimensions={0} | all-to-all | bytes 4194304 | tf_op jit(solution)/shard_map/all_to_all | solution.py:35
  81.1 1.9 reduce_sum.247
  83.0 1.7 collective-permute-start
  84.7 6.3 collective-permute-done
  91.2 2.3 fusion.94
  94.2 4.2 all-to-all-start.2
  99.0 7.1 all-to-all-done.2
  143.8 1.0 fusion.95
  145.3 32.5 %all_to_all.77 = bf16[32,8,4096]{2,1,0:T(8,128)(2,1)S(1)} all-to-all(bf16[32,8,4096]{2,1,0:T(8,128)(2,1)S(1)} %broadcast_in_dim.26), channel_id=1, replica_groups=mesh['section'=8,'dp'=32] {'dp'}, dimensions={0} | all-to-all | bytes 4194304 | tf_op jit(solution)/shard_map/all_to_all | solution.py:18
  177.8 1.3 copy-done.3
  179.1 1.8 fusion.26
  180.9 7.4 %fusion.1 = bf16[32,8,4096]{2,1,0:T(8,128)(2,1)} fusion(bf16[1,344,4096]{2,1,0:T(8,128)(2,1)S(1)} %copy-done, bf16[1,4096,344]{1,2,0:T(8,128)(2,1)} %param.37, bf16[32,8,4096]{2,1,0:T(8,128)(2,1)} %copy-done.3, f32[256,344]{0,1:T(8,128)} %fusion.26), kind=kOutput, calls=%fused_computation.6 | convolution fusion | flops 1444417536 | bytes 10182656 | tf_op jit(solution)/shard_map/dot_general | solution.py:103
  188.3 32.1 %all_to_all.78 = bf16[32,8,4096]{2,1,0:T(8,128)(2,1)S(1)} all-to-all(bf16[32,8,4096]{2,1,0:T(8,128)(2,1)} %fusion.1), channel_id=1, replica_groups=mesh['section'=8,'dp'=32] {'dp'}, dimensions={0} | all-to-all | bytes 4194304 | tf_op jit(solution)/shard_map/all_to_all | solution.py:35
  220.9 1.0 copy-done.1
  221.9 1.0 copy.66
  222.9 2.6 collective-permute-done.1
  225.8 3.6 scatter.49
  229.3 4.0 fusion.93
  234.0 4.6 all-to-all-start.5
  239.5 3.5 scatter.50
  243.0 3.3 all-to-all-done.5
  283.1 2.2 fusion.183
  285.8 32.5 %all_to_all.79 = bf16[32,8,4096]{2,1,0:T(8,128)(2,1)S(1)} all-to-all(bf16[32,8,4096]{2,1,0:T(8,128)(2,1)S(1)} %broadcast_in_dim.28), channel_id=1, replica_groups=mesh['section'=8,'dp'=32] {'dp'}, dimensions={0} | all-to-all | bytes 4194304 | tf_op jit(solution)/shard_map/all_to_all | solution.py:18
  318.3 1.3 copy-done.4
  319.6 1.8 fusion.24
  321.4 7.4 %fusion.2 = bf16[32,8,4096]{2,1,0:T(8,128)(2,1)} fusion(bf16[1,344,4096]{2,1,0:T(8,128)(2,1)S(1)} %copy-done, bf16[1,4096,344]{1,2,0:T(8,128)(2,1)} %param.37, bf16[32,8,4096]{2,1,0:T(8,128)(2,1)} %copy-done.4, f32[256,344]{0,1:T(8,128)} %fusion.24), kind=kOutput, calls=%fused_computation.7 | convolution fusion | flops 1444417536 | bytes 10182656 | tf_op jit(solution)/shard_map/dot_general | solution.py:103
  328.8 32.1 %all_to_all.80 = bf16[32,8,4096]{2,1,0:T(8,128)(2,1)S(1)} all-to-all(bf16[32,8,4096]{2,1,0:T(8,128)(2,1)} %fusion.2), channel_id=1, replica_groups=mesh['section'=8,'dp'=32] {'dp'}, dimensions={0} | all-to-all | bytes 4194304 | tf_op jit(solution)/shard_map/all_to_all | solution.py:35
  361.3 4.7 collective-permute-done.2
  366.3 3.6 scatter.51
  369.9 4.0 fusion.92
  374.6 4.6 all-to-all-start.8
  380.0 3.5 scatter.54
  383.6 3.3 all-to-all-done.8
  423.6 2.2 fusion.181
  426.3 32.5 %all_to_all.81 = bf16[32,8,4096]{2,1,0:T(8,128)(2,1)S(1)} all-to-all(bf16[32,8,4096]{2,1,0:T(8,128)(2,1)S(1)} %broadcast_in_dim.30), channel_id=1, replica_groups=mesh['section'=8,'dp'=32] {'dp'}, dimensions={0} | all-to-all | bytes 4194304 | tf_op jit(solution)/shard_map/all_to_all | solution.py:18
  458.8 1.3 copy-done.5
  460.2 1.8 fusion.22
  462.0 7.4 %fusion.3 = bf16[32,8,4096]{2,1,0:T(8,128)(2,1)} fusion(bf16[1,344,4096]{2,1,0:T(8,128)(2,1)S(1)} %copy-done, bf16[1,4096,344]{1,2,0:T(8,128)(2,1)} %param.37, bf16[32,8,4096]{2,1,0:T(8,128)(2,1)} %copy-done.5, f32[256,344]{0,1:T(8,128)} %fusion.22), kind=kOutput, calls=%fused_computation.8 | convolution fusion | flops 1444417536 | bytes 10182656 | tf_op jit(solution)/shard_map/dot_general | solution.py:103
  469.4 32.1 %all_to_all.82 = bf16[32,8,4096]{2,1,0:T(8,128)(2,1)S(1)} all-to-all(bf16[32,8,4096]{2,1,0:T(8,128)(2,1)} %fusion.3), channel_id=1, replica_groups=mesh['section'=8,'dp'=32] {'dp'}, dimensions={0} | all-to-all | bytes 4194304 | tf_op jit(solution)/shard_map/all_to_all | solution.py:35
  501.9 4.7 collective-permute-done.3
  506.9 3.6 scatter.55
  510.4 4.0 fusion.91
  515.1 4.6 all-to-all-start.11
  520.6 3.5 scatter.56
  524.1 3.3 all-to-all-done.11
  564.7 2.2 fusion.179
  567.4 32.5 %all_to_all.83 = bf16[32,8,4096]{2,1,0:T(8,128)(2,1)S(1)} all-to-all(bf16[32,8,4096]{2,1,0:T(8,128)(2,1)S(1)} %broadcast_in_dim.32), channel_id=1, replica_groups=mesh['section'=8,'dp'=32] {'dp'}, dimensions={0} | all-to-all | bytes 4194304 | tf_op jit(solution)/shard_map/all_to_all | solution.py:18
  600.0 1.3 copy-done.6
  601.3 1.0 fusion.20
  602.3 7.4 %fusion.4 = bf16[32,8,4096]{2,1,0:T(8,128)(2,1)} fusion(bf16[1,344,4096]{2,1,0:T(8,128)(2,1)S(1)} %copy-done, bf16[1,4096,344]{1,2,0:T(8,128)(2,1)} %param.37, bf16[32,8,4096]{2,1,0:T(8,128)(2,1)} %copy-done.6, f32[256,344]{0,1:T(8,128)S(1)} %fusion.20), kind=kOutput, calls=%fused_computation.9 | convolution fusion | flops 1444417536 | bytes 10182656 | tf_op jit(solution)/shard_map/dot_general | solution.py:103
  609.7 4.5 all-to-all-start.13
  615.3 27.4 %all-to-all-done.13 = bf16[32,8,4096]{2,1,0:T(8,128)(2,1)} async-done(((bf16[32,8,4096]{2,1,0:T(8,128)(2,1)}), bf16[32,8,4096]{2,1,0:T(8,128)(2,1)}, u32[]{:S(2)}, u32[]{:S(2)}) %all-to-all-start.13) | async-done | bytes 2097184 | tf_op jit(solution)/shard_map/all_to_all | solution.py:35
  642.7 1.9 convert_reduce_fusion
  644.9 4.2 collective-permute-done.4
  649.3 3.6 scatter.59
  652.9 4.0 fusion.90
  657.6 5.5 all-to-all-start.14
  663.2 3.5 scatter.60
  666.8 4.1 all-to-all-done.14
  708.4 2.2 fusion.177
  (133 shorter events, 26.1 us)
Async XLA Ops:
  0.6 40.3 %copy-start = (bf16[1,344,4096]{2,1,0:T(8,128)(2,1)S(1)}, bf16[1,344,4096]{2,1,0:T(8,128)(2,1)}, u32[]{:S(2)}) copy-start(bf16[1,344,4096]{2,1,0:T(8,128)(2,1)} %param.38) | copy-start | bytes 8454148
  1.8 38.1 %copy-start.9 = (bf16[1,4096,344]{1,2,0:T(8,128)(2,1)S(1)}, bf16[1,4096,344]{1,2,0:T(8,128)(2,1)}, u32[]{:S(2)}) copy-start(bf16[1,4096,344]{1,2,0:T(8,128)(2,1)} %param.36) | copy-start | bytes 8454148
  38.6 1.3 copy-start.2
  81.1 9.9 %copy-start.7 = (bf16[1,8,4096]{2,1,0:T(8,128)(2,1)S(1)}, bf16[1,8,4096]{2,1,0:T(8,128)(2,1)}, u32[]{:S(2)}) copy-start(bf16[1,8,4096]{2,1,0:T(8,128)(2,1)} %param.35) | copy-start | bytes 196612
  81.1 63.9 %copy-start.8 = (f32[1,4096]{1,0:T(1,128)S(1)}, f32[1,4096]{1,0:T(1,128)}, u32[]{:S(2)}) copy-start(f32[1,4096]{1,0:T(1,128)} %param.39) | copy-start | bytes 49156
  83.0 8.0 %collective-permute-start = (bf16[8,4096]{1,0:T(8,128)(2,1)S(1)}, bf16[8,4096]{1,0:T(8,128)(2,1)S(1)}, u32[]{:S(2)}, u32[]{:S(2)}) collective-permute-start(bf16[8,4096]{1,0:T(8,128)(2,1)S(1)} %reduce_sum.247), channel_id=1, source_target_pairs={{0,32},{32,64},{64,96},{96,128},{128,160},{160,192},{192,224},{224... | collective-permute-start | bytes 196616 | tf_op jit(solution)/shard_map/ppermute | solution.py:41
  94.2 12.0 %all-to-all-start.2 = ((f32[32,5,5]{2,1,0:T(8,128)}), f32[32,5,5]{2,1,0:T(8,128)S(1)}, u32[]{:S(2)}, u32[]{:S(2)}) async-start(f32[32,5,5]{2,1,0:T(8,128)} %broadcast_in_dim.25), calls=%async_computation.2 | async-start | bytes 262144 | tf_op jit(solution)/shard_map/all_to_all | solution.py:18
  145.3 33.8 %copy-start.10 = (bf16[1,4096,344]{1,2,0:T(8,128)(2,1)S(1)}, bf16[1,4096,344]{1,2,0:T(8,128)(2,1)}, u32[]{:S(2)}) copy-start(bf16[1,4096,344]{1,2,0:T(8,128)(2,1)} %param.36) | copy-start | bytes 8454148
  177.8 1.4 copy-start.3
  220.7 4.8 collective-permute-start.1
  220.9 1.0 copy-start.1
  234.0 12.3 %all-to-all-start.5 = ((f32[32,5,5]{2,1,0:T(8,128)}), f32[32,5,5]{2,1,0:T(8,128)S(1)}, u32[]{:S(2)}, u32[]{:S(2)}) async-start(f32[32,5,5]{2,1,0:T(8,128)} %broadcast_in_dim.27), calls=%async_computation.5 | async-start | bytes 262144 | tf_op jit(solution)/shard_map/all_to_all | solution.py:18
  285.8 33.8 %copy-start.11 = (bf16[1,4096,344]{1,2,0:T(8,128)(2,1)S(1)}, bf16[1,4096,344]{1,2,0:T(8,128)(2,1)}, u32[]{:S(2)}) copy-start(bf16[1,4096,344]{1,2,0:T(8,128)(2,1)} %param.36) | copy-start | bytes 8454148
  318.3 1.4 copy-start.4
  361.2 4.8 collective-permute-start.2
  374.6 12.3 %all-to-all-start.8 = ((f32[32,5,5]{2,1,0:T(8,128)}), f32[32,5,5]{2,1,0:T(8,128)S(1)}, u32[]{:S(2)}, u32[]{:S(2)}) async-start(f32[32,5,5]{2,1,0:T(8,128)} %broadcast_in_dim.29), calls=%async_computation.8 | async-start | bytes 262144 | tf_op jit(solution)/shard_map/all_to_all | solution.py:18
  426.3 33.9 %copy-start.12 = (bf16[1,4096,344]{1,2,0:T(8,128)(2,1)S(1)}, bf16[1,4096,344]{1,2,0:T(8,128)(2,1)}, u32[]{:S(2)}) copy-start(bf16[1,4096,344]{1,2,0:T(8,128)(2,1)} %param.36) | copy-start | bytes 8454148
  458.8 1.4 copy-start.5
  501.8 4.8 collective-permute-start.3
  515.1 12.3 %all-to-all-start.11 = ((f32[32,5,5]{2,1,0:T(8,128)}), f32[32,5,5]{2,1,0:T(8,128)S(1)}, u32[]{:S(2)}, u32[]{:S(2)}) async-start(f32[32,5,5]{2,1,0:T(8,128)} %broadcast_in_dim.31), calls=%async_computation.11 | async-start | bytes 262144 | tf_op jit(solution)/shard_map/all_to_all | solution.py:18
  567.4 33.8 %copy-start.13 = (bf16[1,4096,344]{1,2,0:T(8,128)(2,1)S(1)}, bf16[1,4096,344]{1,2,0:T(8,128)(2,1)}, u32[]{:S(2)}) copy-start(bf16[1,4096,344]{1,2,0:T(8,128)(2,1)} %param.36) | copy-start | bytes 8454148
  600.0 1.3 copy-start.6
  609.7 33.0 %all-to-all-start.13 = ((bf16[32,8,4096]{2,1,0:T(8,128)(2,1)}), bf16[32,8,4096]{2,1,0:T(8,128)(2,1)}, u32[]{:S(2)}, u32[]{:S(2)}) async-start(bf16[32,8,4096]{2,1,0:T(8,128)(2,1)} %fusion.4), calls=%async_computation.13 | async-start | bytes 4194304 | tf_op jit(solution)/shard_map/all_to_all | solution.py:35
  644.7 4.4 collective-permute-start.4
  657.6 13.3 %all-to-all-start.14 = ((f32[32,5,5]{2,1,0:T(8,128)}), f32[32,5,5]{2,1,0:T(8,128)S(1)}, u32[]{:S(2)}, u32[]{:S(2)}) async-start(f32[32,5,5]{2,1,0:T(8,128)} %broadcast_in_dim.33), calls=%async_computation.14 | async-start | bytes 262144 | tf_op jit(solution)/shard_map/all_to_all | solution.py:18
where the time goes:
time: 724 us; the launch traced here: 712 us
  blocking collectives  296 us (41%)
  between operations  176 us (24%)
  matrix products  72.7 us (10%)
  waiting for transfers between devices  71.1 us (10%)
  local copies, waits for them, and re-layouts  55.4 us (8%)
  starting transfers between devices  30.2 us (4%)
  other arithmetic  11.1 us (2%)
    all_to_all x5, blocking collectives, copy_for_each(): lax.all_to_all(jnp.broadcast_to(array[None], (peers, *array.shape)), axis...  167 us
    all_to_all x4, blocking collectives, sent_and_summed(): tiles = lax.all_to_all(split_up(array, dim, peers), axis, 0, 0, tiled=True)  129 us
    dot_general x5, matrix products, local(): partials = jnp.dot(hidden, down_local, preferred_element_type=jnp.float32)  37 us
    all_to_all x1, waiting for transfers between devices, sent_and_summed(): tiles = lax.all_to_all(split_up(array, dim, peers), axis, 0, 0, tiled=True)  27.4 us
    all_to_all x5, starting transfers between devices, copy_for_each(): lax.all_to_all(jnp.broadcast_to(array[None], (peers, *array.shape)), axis...  23.6 us
    ppermute x5, waiting for transfers between devices, passed_along(): lax.ppermute(array, axis, [(i, (i + by) % peers) for i in range(peers)])  22.6 us
    all_to_all x5, waiting for transfers between devices, copy_for_each(): lax.all_to_all(jnp.broadcast_to(array[None], (peers, *array.shape)), axis...  21.2 us
    dot_general x5, matrix products, local(): jnp.einsum('htd,gtd->hg', misfits, misfits, precision=lax.Precision.HIGHEST)  18.4 us
  transfers between devices with their start and end apart: 11, of which 11 were waited for; matrix products, arithmetic and copies ran while one was open for 3% of the time, Pallas kernels for 0%

commit v1 on v0

v1 whole, which is shorter than its diff:
```python
import functools
import math

import jax
import jax.numpy as jnp
from jax import lax
from jax.experimental import pallas as pl
from jax.experimental.pallas import tpu as pltpu
from jax.sharding import PartitionSpec as P

ITERS = 5
HIST = 5
BF = jnp.bfloat16
F32 = jnp.float32
MESH = pl.DeviceIdType.MESH
PIECES = 4


def solve_small(entries, values):
    count = len(values)
    entries = [list(row) for row in entries]
    values = list(values)
    for p in range(count):
        for i in range(p + 1, count):
            factor = entries[i][p] / entries[p][p]
            for j in range(p, count):
                entries[i][j] = entries[i][j] - factor * entries[p][j]
            values[i] = values[i] - factor * values[p]
    answer = [None] * count
    for i in range(count - 1, -1, -1):
        accum = values[i]
        for j in range(i + 1, count):
            accum = accum - entries[i][j] * answer[j]
        answer[i] = accum / entries[i][i]
    return answer


def kernel(
    dims,
    inject_hbm, gate_hbm, up_hbm, down_hbm, gain_hbm,
    out_ref, mix_ref,
    wg_v, wu_v, wgu, wd, inj_v, gain_v,
    images, misfits, x_v, prod, rows_sq, gram, mixes,
    ybuf, meta, hid, part, r1, s2, r2, xr, xf,
    load_sem, init_send, init_recv,
    p1_send, p1_recv, p2_send, p2_recv, x_send, x_recv, h_send, h_recv,
    a1_send, a1_recv, a2_send, a2_recv, fw_send, fw_recv,
    m1_send, m1_recv, m2_send, m2_recv, mf_send, mf_recv, o_send, o_recv,
):
    n, ns, tok, feat, units, pad = dims
    rows = 2 * tok
    half = feat // 2
    width = half // PIECES
    total_rows = n * n * rows
    cells = float(total_rows * feat)
    s = lax.axis_index("section")
    d = lax.axis_index("dp")
    c = lax.rem(d, 2)
    y = lax.rem(d // 2, n)
    x = d // (2 * n)
    other = 1 - c
    below = lax.rem(s + 1, ns)
    above = lax.rem(s + ns - 1, ns)

    def at(sec, xx, yy, cc):
        return (sec, (xx * n + yy) * 2 + cc)

    def ring(i, by):
        return lax.rem(i + by, n)

    partner = at(s, x, y, other)
    along_x = [at(s, ring(x, k), y, c) for k in range(1, n)]
    along_y = [at(s, x, ring(y, k), c) for k in range(1, n)]

    def send(src, dst, ssem, rsem, dev):
        cp = pltpu.make_async_remote_copy(
            src_ref=src, dst_ref=dst, send_sem=ssem, recv_sem=rsem,
            device_id=dev, device_id_type=MESH,
        )
        cp.start()

    def wait(ref, sem):
        pltpu.make_async_copy(ref, ref, sem).wait()

    mine = pl.ds(pl.multiple_of(c * half, 128), half)
    theirs = pl.ds(pl.multiple_of(other * half, 128), half)
    own_tok = pl.ds(pl.multiple_of(c * tok, 8), tok)
    own_units = pl.ds(pl.multiple_of(c * pad, 128), units)
    loads = [
        pltpu.make_async_copy(inject_hbm.at[0, :, mine], inj_v.at[own_tok, :], load_sem.at[0]),
        pltpu.make_async_copy(gain_hbm.at[:, mine], gain_v, load_sem.at[1]),
        pltpu.make_async_copy(gate_hbm.at[0], wg_v, load_sem.at[2]),
        pltpu.make_async_copy(up_hbm.at[0], wu_v, load_sem.at[3]),
        pltpu.make_async_copy(down_hbm.at[0, :, mine], wd.at[own_units, :], load_sem.at[4]),
    ]
    for cp in loads:
        cp.start()

    barrier = pltpu.get_barrier_semaphore()
    sources = (
        [partner]
        + along_x
        + along_y
        + [at(above, xx, y, c) for xx in [ring(x, k) for k in range(n)]]
        + [at(above, x, yy, c) for yy in [ring(y, k) for k in range(1, n)]]
    )
    for dev in sources:
        pl.semaphore_signal(barrier, inc=1, device_id=dev, device_id_type=MESH)
    pl.semaphore_wait(barrier, len(sources))

    send(inject_hbm.at[0, :, theirs], inj_v.at[own_tok, :], init_send.at[0], init_recv.at[0], partner)
    send(down_hbm.at[0, :, theirs], wd.at[own_units, :], init_send.at[1], init_recv.at[1], partner)

    images[...] = jnp.zeros_like(images)
    misfits[...] = jnp.zeros_like(misfits)
    rows_sq[...] = jnp.zeros_like(rows_sq)
    gram[...] = jnp.zeros_like(gram)
    mixes[...] = jnp.zeros_like(mixes)

    lane = lax.broadcasted_iota(jnp.int32, (rows, 128), 1)
    lane8 = lax.broadcasted_iota(jnp.int32, (8, 128), 1)

    def x_first(q):
        return q % 2 == 0

    def gather_start(slot, q):
        piece = ybuf.at[slot, c, q, x, y]
        for dev in along_x if x_first(q) else along_y:
            send(piece, piece, a1_send.at[q], a1_recv.at[slot, q], dev)

    def line(slot, q):
        return ybuf.at[slot, c, q, :, y] if x_first(q) else ybuf.at[slot, c, q, x]

    def meta_start(slot):
        piece = meta.at[slot, c, x, y]
        for dev in along_x:
            send(piece, piece, m1_send, m1_recv.at[slot], dev)

    def new_image(slot, q, out_piece):
        cols = pl.ds(q * width, width)
        image = inj_v[:, cols].astype(F32) + 0.5 * out_piece
        misfit = image - x_v[:, cols]
        images[slot, :, cols] = image
        misfits[slot, :, cols] = misfit
        ybuf[slot_y(slot), c, q, x, y] = (image * gain_v[0:1, cols]).astype(BF)
        return image, misfit

    def slot_y(slot):
        return jnp.minimum(slot, ITERS - 1) if not isinstance(slot, int) else slot

    def folded(v):
        acc = v[:, 0:128]
        for g in range(1, width // 128):
            acc = acc + v[:, g * 128 : (g + 1) * 128]
        return acc

    def products(q, image, misfit, sums):
        cols = pl.ds(q * width, width)
        new = []
        for j in range(HIST):
            new.append(folded(image * images[j, :, cols]))
            new.append(folded(misfit * misfits[j, :, cols]))
        return new if sums is None else [a + b for a, b in zip(sums, new)]

    def meta_tile(slot, sums):
        tile = jnp.zeros((rows, 128), F32)
        for j in range(HIST):
            tile = tile + jnp.where(lane == j, jnp.sum(sums[2 * j], axis=1, keepdims=True), 0.0)
            tile = tile + jnp.where(lane == 8 + j, jnp.sum(sums[2 * j + 1], axis=1, keepdims=True), 0.0)
        meta[slot, c, x, y] = tile

    def meta_second(slot):
        wait(r_meta(slot), m1_recv.at[slot])
        group = meta.at[slot, c, :, y]
        for dev in along_y:
            send(group, group, m2_send, m2_recv.at[slot], dev)

    def r_meta(slot):
        return meta.at[slot, 0, 0, pl.ds(0, n - 1)]

    def meta_third(slot):
        wait(meta.at[slot, 0, pl.ds(0, n - 1)], m2_recv.at[slot])
        whole = meta.at[slot, c]
        send(whole, whole, mf_send, mf_recv.at[slot], partner)

    def meta_done(slot):
        wait(meta.at[slot, 0], mf_recv.at[slot])

    def meta_sends_done(slot):
        wait(r_meta(slot), m1_send)
        wait(meta.at[slot, 0, pl.ds(0, n - 1)], m2_send)
        wait(meta.at[slot, 0], mf_send)

    def mix(slot):
        both = (meta[slot, 0] + meta[slot, 1]).reshape(total_rows, 128)
        rows_sq[slot] = both
        sums = jnp.sum(both.reshape(total_rows // 8, 8, 128), axis=0)
        sums = jnp.broadcast_to(jnp.sum(sums, axis=0, keepdims=True), (8, 128)) / cells
        for j in range(HIST):
            entry = jnp.sum(jnp.where(lane8 == 8 + j, sums, 0.0), axis=1, keepdims=True)
            entry = jnp.broadcast_to(entry, (8, 128))
            gram[slot, j] = entry
            gram[j, slot] = entry
        live = [jnp.where(i <= slot, 1.0, 0.0).astype(F32) for i in range(HIST)]
        matrix = [[gram[i, j] for j in range(HIST)] for i in range(HIST)]
        trace = matrix[0][0]
        for i in range(1, HIST):
            trace = trace + matrix[i][i]
        damp = 0.01 * trace / jnp.full((8, 128), slot + 1, jnp.int32).astype(F32) + 1e-06
        system = [
            [
                matrix[i][j] * (live[i] * live[j])
                + ((live[i] * damp + (1.0 - live[i])) if i == j else 0.0)
                for j in range(HIST)
            ]
            for i in range(HIST)
        ]
        beta = solve_small(system, [jnp.full((8, 128), live[i], F32) for i in range(HIST)])
        norm = beta[0]
        for i in range(1, HIST):
            norm = norm + beta[i]
        weights = [b / norm for b in beta]
        row = jnp.zeros((8, 128), F32)
        for i in range(HIST):
            row = row + jnp.where(lane8 == i, weights[i], 0.0)
        mixes[slot] = row
        return weights

    def mixed_images(weights, cols):
        acc = weights[0][0:1, 0:1] * images[0, :, cols]
        for i in range(1, HIST):
            acc = acc + weights[i][0:1, 0:1] * images[i, :, cols]
        return acc

    loads[0].wait()
    loads[1].wait()
    wait(inj_v.at[own_tok, :], init_recv.at[0])
    x_v[...] = jnp.zeros_like(x_v)
    sums = None
    for q in range(PIECES):
        image, misfit = new_image(0, q, jnp.zeros((rows, width), F32))
        gather_start(0, q)
        sums = products(q, image, misfit, sums)
    meta_tile(0, sums)
    meta_start(0)

    loads[2].wait()
    loads[3].wait()
    step = 256

    def place(i, _):
        at_rows = pl.ds(pl.multiple_of(i * step, step), step)
        zeros = jnp.zeros((step, pad - units), BF)
        wgu[at_rows, 0:units] = wg_v[at_rows, :]
        wgu[at_rows, units:pad] = zeros
        wgu[at_rows, pad : pad + units] = wu_v[at_rows, :]
        wgu[at_rows, pad + units : 2 * pad] = zeros
        return 0

    lax.fori_loop(0, feat // step, place, 0)
    wd[units:pad, :] = jnp.zeros((pad - units, half), BF)
    wd[pad + units : 2 * pad, :] = jnp.zeros((pad - units, half), BF)
    prod[...] = jnp.zeros_like(prod)
    loads[4].wait()
    wait(wd.at[own_units, :], init_recv.at[1])
    wait(inj_v.at[own_tok, :], init_send.at[0])
    wait(wd.at[own_units, :], init_send.at[1])

    def matmul(slot, side, q, first):
        at_rows = pl.ds(pl.multiple_of(side * half + q * width, width), width)
        lhs = ybuf[slot, side, q].reshape(total_rows, width)
        got = jnp.dot(lhs, wgu[at_rows, :], preferred_element_type=F32)
        if first:
            prod[slot] = got
        else:
            prod[slot] += got

    def body(k, _):
        for q in range(PIECES):
            wait(ybuf.at[k, 0, 0, 0, pl.ds(0, n - 1)], a1_recv.at[k, q])
            group = line(k, q)
            for dev in along_y if x_first(q) else along_x:
                send(group, group, a2_send.at[q], a2_recv.at[k, q], dev)
        meta_second(k)
        for q in range(PIECES):
            wait(ybuf.at[k, 0, 0, pl.ds(0, n - 1)], a2_recv.at[k, q])
            whole = ybuf.at[k, c, q]
            send(whole, whole, fw_send.at[q], fw_recv.at[k, q], partner)
            if q == PIECES - 2:
                meta_third(k)
            matmul(k, c, q, q == 0)
        for q in range(PIECES - 1):
            wait(ybuf.at[k, 0, 0], fw_recv.at[k, q])
            matmul(k, other, q, False)
        for q in range(PIECES):
            wait(ybuf.at[k, 0, 0, 0, pl.ds(0, n - 1)], a1_send.at[q])
        meta_done(k)
        weights = mix(k)
        for q in range(PIECES):
            cols = pl.ds(q * width, width)
            x_v[:, cols] = mixed_images(weights, cols)
        send(x_v, xr.at[k], x_send, x_recv.at[k], at(below, x, y, c))
        acc = jnp.zeros((total_rows // 8, 8, 128), F32)
        for i in range(ITERS - 1):
            vec = jnp.zeros((8, 128), F32)
            for j in range(i + 1):
                vec = vec + jnp.where(lane8 == j, weights[j] * (1.0 if j == i else 2.0), 0.0)
            acc = acc + rows_sq[i].reshape(total_rows // 8, 8, 128) * (weights[i] * vec)[None]
        mean_sq = jnp.sum(acc.reshape(total_rows, 128), axis=1, keepdims=True) / float(feat)
        xf[...] = jnp.broadcast_to(
            lax.rsqrt(jnp.maximum(mean_sq, 0.0) + 1e-06), (total_rows, 128)
        )
        wait(ybuf.at[k, 0, 0], fw_recv.at[k, PIECES - 1])
        matmul(k, other, PIECES - 1, False)

        group_rows = 64
        own_hid = pl.ds(pl.multiple_of(c * pad, 128), pad)

        def hidden(i, _):
            at_rows = pl.ds(pl.multiple_of(i * group_rows, group_rows), group_rows)
            scale = xf[at_rows, 0:1]

            def mixed(first):
                got = weights[0][0:1, 0:1] * prod[0, at_rows, pl.ds(first, pad)]
                for j in range(1, ITERS - 1):
                    got = got + weights[j][0:1, 0:1] * prod[j, at_rows, pl.ds(first, pad)]
                return got * scale

            gate = mixed(0)
            up = mixed(pad)
            hid[at_rows, own_hid] = (gate / (1.0 + jnp.exp(-gate)) * up).astype(BF)
            return 0

        lax.fori_loop(0, total_rows // group_rows, hidden, 0)
        send(hid.at[:, own_hid], hid.at[:, own_hid], h_send, h_recv.at[k], partner)
        wait(hid.at[:, own_hid], h_recv.at[k])

        for q in range(PIECES):
            got = jnp.dot(hid[...], wd[:, q * width : (q + 1) * width], preferred_element_type=F32)
            part[q] = got.astype(BF).reshape(n, n, rows, width)
            for g in range(1, n):
                if x_first(q):
                    yy = ring(y, g)
                    src, dev = part.at[q, :, yy], at(s, x, yy, c)
                else:
                    xx = ring(x, g)
                    src, dev = part.at[q, xx], at(s, xx, y, c)
                send(src, r1.at[k, q, g - 1], p1_send.at[q], p1_recv.at[k, q], dev)
        for q in range(PIECES):
            wait(r1.at[k, q], p1_recv.at[k, q])
            own = part[q, :, y] if x_first(q) else part[q, x]
            got = own.astype(F32)
            for g in range(n - 1):
                got = got + r1[k, q, g].astype(F32)
            s2[q] = got.astype(BF)
            for g in range(n):
                if x_first(q):
                    dst, dev, place_at = ring(x, g), at(below, ring(x, g), y, c), x
                else:
                    dst, dev, place_at = ring(y, g), at(below, x, ring(y, g), c), y
                send(s2.at[q, dst], r2.at[k, q, place_at], p2_send.at[q], p2_recv.at[k, q], dev)
        wait(xr.at[k], x_recv.at[k])
        sums = None
        for q in range(PIECES):
            cols = pl.ds(q * width, width)
            wait(r2.at[k, q], p2_recv.at[k, q])
            got = r2[k, q, 0].astype(F32)
            for g in range(1, n):
                got = got + r2[k, q, g].astype(F32)
            out = (xr[k, :, cols] + got).astype(BF).astype(F32)
            image, misfit = new_image(k + 1, q, out)

            @pl.when(k < ITERS - 2)
            def _():
                gather_start(k + 1, q)

            sums = products(q, image, misfit, sums)
        meta_tile(k + 1, sums)

        for q in range(PIECES):
            wait(ybuf.at[k, 0, 0, pl.ds(0, n - 1)], a2_send.at[q])
            wait(ybuf.at[k, 0, 0], fw_send.at[q])
            wait(r1.at[k, q], p1_send.at[q])
            wait(r2.at[k, q], p2_send.at[q])
        meta_sends_done(k)
        wait(xr.at[k], x_send)
        wait(hid.at[:, own_hid], h_send)
        meta_start(k + 1)
        return 0

    def run(k, carry):
        return body(k, carry)

    lax.fori_loop(0, ITERS - 1, run, 0)

    last = ITERS - 1
    meta_second(last)
    meta_third(last)
    meta_done(last)
    weights = mix(last)
    for q in range(PIECES):
        cols = pl.ds(q * width, width)
        x_v[:, cols] = mixed_images(weights, cols)
    their_tok = pl.ds(pl.multiple_of(other * tok, 8), tok)
    send(x_v.at[their_tok, :], out_ref.at[0, :, mine], o_send, o_recv, partner)
    out_ref[0, :, mine] = x_v[own_tok, :]
    for i in range(ITERS):
        mix_ref[0, i : i + 1, :] = mixes[i, 0:1, 0:HIST]
    meta_sends_done(last)
    wait(x_v.at[their_tok, :], o_recv)
    wait(x_v.at[their_tok, :], o_send)


def local(inject, w_gate, w_up, w_down, gain):
    ns = lax.axis_size("section")
    ndp = lax.axis_size("dp")
    n = math.isqrt(ndp // 2)
    tok, feat = inject.shape[1], inject.shape[2]
    units = w_gate.shape[2]
    pad = -(-units // 128) * 128
    rows, half = 2 * tok, feat // 2
    width = half // PIECES
    total_rows = n * n * rows
    dims = (n, ns, tok, feat, units, pad)
    any_space = pl.BlockSpec(memory_space=pl.ANY)
    vmem = pl.BlockSpec(memory_space=pltpu.VMEM)
    dma = pltpu.SemaphoreType.DMA
    steps = ITERS - 1
    return pl.pallas_call(
        functools.partial(kernel, dims),
        name="fixed_point",
        out_shape=(
            jax.ShapeDtypeStruct((1, tok, feat), F32),
            jax.ShapeDtypeStruct((1, ITERS, HIST), F32),
        ),
        in_specs=[any_space] * 5,
        out_specs=(vmem, vmem),
        scratch_shapes=[
            pltpu.VMEM((feat, units), BF),
            pltpu.VMEM((feat, units), BF),
            pltpu.VMEM((feat, 2 * pad), BF),
            pltpu.VMEM((2 * pad, half), BF),
            pltpu.VMEM((rows, half), BF),
            pltpu.VMEM((1, half), F32),
            pltpu.VMEM((HIST, rows, half), F32),
            pltpu.VMEM((HIST, rows, half), F32),
            pltpu.VMEM((rows, half), F32),
            pltpu.VMEM((steps, total_rows, 2 * pad), F32),
            pltpu.VMEM((HIST, total_rows, 128), F32),
            pltpu.VMEM((HIST, HIST, 8, 128), F32),
            pltpu.VMEM((ITERS, 8, 128), F32),
            pltpu.VMEM((ITERS, 2, PIECES, n, n, rows, width), BF),
            pltpu.VMEM((ITERS, 2, n, n, rows, 128), F32),
            pltpu.VMEM((total_rows, 2 * pad), BF),
            pltpu.VMEM((PIECES, n, n, rows, width), BF),
            pltpu.VMEM((steps, PIECES, n - 1, n, rows, width), BF),
            pltpu.VMEM((PIECES, n, rows, width), BF),
            pltpu.VMEM((steps, PIECES, n, rows, width), BF),
            pltpu.VMEM((steps, rows, half), F32),
            pltpu.VMEM((total_rows, 128), F32),
            dma((5,)), dma((2,)), dma((2,)),
            dma((PIECES,)), dma((steps, PIECES)),
            dma((PIECES,)), dma((steps, PIECES)),
            dma(()), dma((steps,)),
            dma(()), dma((steps,)),
            dma((PIECES,)), dma((steps, PIECES)),
            dma((PIECES,)), dma((steps, PIECES)),
            dma((PIECES,)), dma((steps, PIECES)),
            dma(()), dma((ITERS,)),
            dma(()), dma((ITERS,)),
            dma(()), dma((ITERS,)),
            dma(()), dma(()),
        ],
        compiler_params=pltpu.CompilerParams(
            collective_id=0, has_side_effects=True, vmem_limit_bytes=63 << 20
        ),
    )(inject, w_gate, w_up, w_down, gain)


def solution(mesh):
    placed = (
        P("section", "dp", None),
        P("section", None, "dp"),
        P("section", None, "dp"),
        P("section", "dp", None),
        P("section", None),
    )
    return jax.shard_map(
        local,
        mesh=mesh,
        in_specs=placed,
        out_specs=(P("section", "dp", None), P("section", None, None)),
        check_vma=False,
    )
```

time: 724 us -> 153 us (0.21); the launches traced: 712 us -> 153 us
  blocking collectives: 296 us -> 0 us
  between operations: 176 us -> 0.65 us
  Pallas kernels: 0 us -> 142 us
  matrix products: 72.7 us -> 0 us
  waiting for transfers between devices: 71.1 us -> 0 us
  local copies, waits for them, and re-layouts: 55.4 us -> 10.3 us
  starting transfers between devices: 30.2 us -> 0 us
  other arithmetic: 11.1 us -> 0 us
    all_to_all x9 -> x0, blocking collectives: 296 us -> none  [the longest x5 167 us: copy_for_each(): lax.all_to_all(jnp.broadcast_to(array[None], (peers, *array.shape)), axis...]
    pallas_call x0 -> x1, Pallas kernels: none -> 142 us  [local(): pl.pallas_call(functools.partial(kernel, dims), name='fixed_point', out_s...]
    dot_general x20 -> x0, matrix products: 72.7 us -> none  [the longest x5 37 us: local(): partials = jnp.dot(hidden, down_local, preferred_element_type=jnp.float32)]
    all_to_all x6 -> x0, waiting for transfers between devices: 48.6 us -> none  [the longest x1 27.4 us: sent_and_summed(): tiles = lax.all_to_all(split_up(array, dim, peers), axis, 0, 0, tiled=True)]
    scatter x13 -> x0, local copies, waits for them, and re-layouts: 28.6 us -> none  [the longest x5 14.3 us: local(): misfits = misfits.at[iteration].set(misfit)]
    all_to_all x6 -> x0, starting transfers between devices: 28.2 us -> none  [the longest x5 23.6 us: copy_for_each(): lax.all_to_all(jnp.broadcast_to(array[None], (peers, *array.shape)), axis...]
    ppermute x5 -> x0, waiting for transfers between devices: 22.6 us -> none  [passed_along(): lax.ppermute(array, axis, [(i, (i + by) % peers) for i in range(peers)])]
    slice x15 -> x0, local copies, waits for them, and re-layouts: 10.2 us -> none  [the longest x10 6.87 us: solve_small(): entries = [[system[..., i, j] for j in range(count)] for i in range(count)]]
  transfers between devices with their start and end apart: 11 -> 0, of which waited for: 11 -> 0; matrix products, arithmetic and copies ran while one was open for 3% -> 0% of each run, Pallas kernels for 0% -> 0%
where the time goes in v1:
time: 153 us
  Pallas kernels  142 us (93%)
  local copies, waits for them, and re-layouts  10.3 us (7%)
    pallas_call x1, Pallas kernels, local(): pl.pallas_call(functools.partial(kernel, dims), name='fixed_point', out_s...  142 us
    unnamed x5, local copies, waits for them, and re-layouts  9.09 us

profile of v1, /device:TPU:1, one launch (start us, length us, event | category | flops | bytes accessed | tf_op | source)
XLA Modules:
  0.0 152.6 jit_solution(12697195305658809868)
XLA Ops:
  0.6 0.0 copy-start
  0.6 4.7 %copy.7.gate_hbm = bf16[1,4096,344]{2,1,0:T(8,128)(2,1)} copy(bf16[1,4096,344]{1,2,0:T(8,128)(2,1)} %param.6) | data formatting | bytes 5636096 | tf_op args[1]
  5.4 0.0 copy-done
  5.4 2.8 %copy.8.up_hbm = bf16[1,4096,344]{2,1,0:T(8,128)(2,1)} copy(bf16[1,4096,344]{1,2,0:T(8,128)(2,1)S(1)} %copy-done) | data formatting | bytes 5636096 | tf_op args[2]
  8.2 141.6 %fixed_point.1 = (f32[1,8,4096]{2,1,0:T(8,128)}, f32[1,5,5]{2,1,0:T(8,128)}) custom-call(bf16[1,8,4096]{2,1,0:T(8,128)(2,1)} %inject_hbm.1, bf16[1,4096,344]{2,1,0:T(8,128)(2,1)} %copy.7.gate_hbm, bf16[1,4096,344]{2,1,0:T(8,128)(2,1)} %copy.8.up_hbm, bf16[1,344,4096]{2,1,0:T(8,128)(2,1)} %down_hbm.1, f32[1,4096]{1,0:T(1,128)} %gain_hbm.1), custom_call_target="tpu_custom_call" | custom-call | tf_op jit(solution)/shard_map/fixed_point/pallas_call | solution.py:429
  149.7 1.3 copy.9
  151.0 1.6 %copy.11 = f32[1,8,4096]{2,1,0:T(8,128)} copy(f32[1,8,4096]{2,1,0:T(8,128)} %get-tuple-element.6) | data formatting | bytes 262144
Async XLA Ops:
  0.6 4.7 %copy-start = (bf16[1,4096,344]{1,2,0:T(8,128)(2,1)S(1)}, bf16[1,4096,344]{1,2,0:T(8,128)(2,1)}, u32[]{:S(2)}) copy-start(bf16[1,4096,344]{1,2,0:T(8,128)(2,1)} %param.7) | copy-start | bytes 8454148
